TPU v7x, 32 devices: a whole 2x2x4 slice. The times are simulated.
32 devices in a mesh: pr: 8 (over y, x, core), pc: 4 (over z).
Axes of the slice: x: 2, y: 2, z: 4, core: 2. Of those that a mesh axis runs over, the one named last changes fastest.
Arguments:
- pair_array: bfloat16 [256, 256, 128], P('pr', 'pc'), may hold values from -6 to 6
- left_weight: bfloat16 [128, 128], replicated, may hold values from -0.5 to 0.5
- right_weight: bfloat16 [128, 128], replicated, may hold values from -0.5 to 0.5
- left_gate: bfloat16 [128, 128], replicated, may hold values from -0.5 to 0.5
- right_gate: bfloat16 [128, 128], replicated, may hold values from -0.5 to 0.5
- mid_gain: float32 [128], replicated, may hold values from 0.25 to 1.75
- out_weight: bfloat16 [128, 128], replicated, may hold values from -0.5 to 0.5
- out_gate: bfloat16 [128, 128], replicated, may hold values from -0.5 to 0.5
Outputs:
- pair_update: bfloat16 [256, 256, 128], P('pr', 'pc')
All inputs are finite; a program needn't handle non-finite values.
Results may differ from a plain program's by a relative error of at most 0.012.
Values may be sent and summed in bfloat16 or wider, within the bound.
A program may use at most 128 MiB of HBM per device.

v0:
```python
import jax
import jax.numpy as jnp
from jax import lax
from jax.sharding import PartitionSpec as P


def unit_channels(values, channel_gain):
    centred = values - jnp.mean(values, axis=-1, keepdims=True)
    return (
        centred
        * lax.rsqrt(jnp.mean(centred * centred, axis=-1, keepdims=True) + 1e-05)
        * channel_gain
    )


def make_factors(pair_in, left_weight, right_weight, left_gate, right_gate):
    left = jnp.einsum("ijc,cd->ijd", pair_in, left_weight, preferred_element_type=jnp.float32)
    left = left * jax.nn.sigmoid(
        jnp.einsum("ijc,cd->ijd", pair_in, left_gate, preferred_element_type=jnp.float32)
    )
    right = jnp.einsum("ijc,cd->ijd", pair_in, right_weight, preferred_element_type=jnp.float32)
    right = right * jax.nn.sigmoid(
        jnp.einsum("ijc,cd->ijd", pair_in, right_gate, preferred_element_type=jnp.float32)
    )
    return (pair_in, left.astype(jnp.bfloat16), right.astype(jnp.bfloat16))


def to_pair(mixed, ready, mid_gain, out_weight, out_gate):
    scaled = unit_channels(mixed.astype(jnp.float32), mid_gain).astype(jnp.bfloat16)
    scaled = lax.optimization_barrier(scaled)
    gate = jax.nn.sigmoid(
        jnp.einsum("ijc,cd->ijd", ready, out_gate, preferred_element_type=jnp.float32)
    )
    return (
        jnp.einsum("ijd,dc->ijc", scaled, out_weight, preferred_element_type=jnp.float32) * gate
    ).astype(jnp.bfloat16)


def on_device(
    pair_array, left_weight, right_weight, left_gate, right_gate, mid_gain, out_weight, out_gate
):
    ready, left, right = make_factors(pair_array, left_weight, right_weight, left_gate, right_gate)
    count = pair_array.shape[0] * lax.axis_size("pr")
    left_lines, right_lines = (
        lax.all_to_all(left, "pr", split_axis=2, concat_axis=0, tiled=True),
        lax.all_to_all(right, "pr", split_axis=2, concat_axis=0, tiled=True),
    )
    strip = jnp.einsum(
        "kid,kjd->ijd",
        lax.all_gather(left_lines, "pc", axis=1, tiled=True),
        right_lines,
        preferred_element_type=jnp.float32,
    )
    strip = (strip * count ** (-0.5)).astype(jnp.bfloat16)
    mixed = lax.all_to_all(strip, "pr", split_axis=0, concat_axis=2, tiled=True)
    return to_pair(mixed, ready, mid_gain, out_weight, out_gate)


def solution(mesh):
    return jax.shard_map(
        on_device,
        mesh=mesh,
        in_specs=(P("pr", "pc", None), P(), P(), P(), P(), P(), P(), P()),
        out_specs=P("pr", "pc", None),
        check_vma=False,
    )
```

profile of v0, /device:TPU:0, one launch (start us, length us, event | category | flops | bytes accessed | tf_op | source)
XLA Modules:
  0.0 104.0 jit_solution(1541400130074911763)
XLA Ops:
  6.5 0.0 copy-start
  6.5 0.0 all-gather.2.cloned.1.call-start
  6.5 1.0 copy-done
  7.6 1.0 fusion.24
  8.6 1.2 %fusion.14 = bf16[32,64,128]{2,1,0:T(8,128)(2,1)S(1)} fusion(f32[32,64,128]{2,1,0:T(8,128)S(1)} %fusion.24, bf16[32,64,128]{2,1,0:T(8,128)(2,1)S(1)} %copy-done, bf16[128,128]{1,0:T(8,128)(2,1)} %param.11), kind=kOutput, calls=%fused_computation.22 | convolution fusion | flops 68419584 | bytes 2129920 | tf_op jit(solution)/shard_map/ijc,cd->ijd/dot_general | solution.py:19
  9.8 1.6 %copy.25 = bf16[32,64,128]{1,0,2:T(8,128)(2,1)S(1)} copy(bf16[32,64,128]{2,1,0:T(8,128)(2,1)S(1)} %fusion.14) | data formatting | bytes 1048576 | tf_op jit(solution)/shard_map/convert_element_type | solution.py:25
  11.4 0.7 reshape.28
  12.2 14.7 %all_to_all.45 = bf16[8,2,16384]{2,1,0:T(2,128)(2,1)S(1)} all-to-all(bf16[8,2,16384]{2,1,0:T(2,128)(2,1)S(1)} %reshape.28), channel_id=1, replica_groups=mesh['pr'=8,'pc'=4] {'pr'}, dimensions={0} | all-to-all | bytes 1048576 | tf_op jit(solution)/shard_map/all_to_all | solution.py:45
  26.8 0.7 reshape.29
  27.5 0.0 copy-start.1
  27.5 0.4 copy.27
  27.9 0.0 copy-start.4
  28.0 1.6 %copy.28 = bf16[256,64,16]{0,1,2:T(8,128)(2,1)} copy(bf16[256,64,16]{1,2,0:T(8,128)(2,1)S(1)} %bitcast.66) | data formatting | bytes 1048576 | tf_op jit(solution)/shard_map/all_to_all | solution.py:45
  29.6 0.0 all-gather.2.cloned.1.call-update
  29.6 0.0 copy-done.1
  29.6 0.3 fusion.27
  29.9 0.0 copy-done.4
  29.9 0.4 fusion.15
  30.4 1.6 %copy.22 = bf16[32,64,128]{1,0,2:T(8,128)(2,1)S(1)} copy(bf16[32,64,128]{2,1,0:T(8,128)(2,1)S(1)} %fusion.15) | data formatting | bytes 1048576 | tf_op jit(solution)/shard_map/convert_element_type | solution.py:25
  32.0 0.7 reshape.30
  32.7 12.1 %all_to_all.46 = bf16[8,2,16384]{2,1,0:T(2,128)(2,1)S(1)} all-to-all(bf16[8,2,16384]{2,1,0:T(2,128)(2,1)S(1)} %reshape.30), channel_id=1, replica_groups=mesh['pr'=8,'pc'=4] {'pr'}, dimensions={0} | all-to-all | bytes 1048576 | tf_op jit(solution)/shard_map/all_to_all | solution.py:46
  44.8 0.7 reshape.31
  45.5 0.4 copy.24
  45.9 28.9 %all-gather.2.cloned.1.call-done = bf16[256,256,16]{0,1,2:T(8,128)(2,1)} async-done(((bf16[256,64,16]{0,1,2:T(8,128)(2,1)}), bf16[256,256,16]{0,1,2:T(8,128)(2,1)}) %all-gather.2.cloned.1.call-update) | async-done | bytes 2097168 | tf_op jit(solution)/shard_map/all_gather | solution.py:50
  74.8 2.4 %fusion.18 = bf16[256,64,16]{0,1,2:T(8,128)(2,1)S(1)} fusion(bf16[256,256,16]{0,1,2:T(8,128)(2,1)} %all-gather.2.cloned.1.call-done, bf16[256,64,16]{1,2,0:T(8,128)(2,1)S(1)} %bitcast.61), kind=kOutput, calls=%fused_computation.26 | convolution fusion | flops 134742016 | bytes 3145728 | tf_op jit(solution)/shard_map/kid,kjd->ijd/dot_general | solution.py:48
  77.2 0.0 copy-start.5
  77.2 1.0 copy.30
  78.1 1.5 %reshape.32 = bf16[8,2,16384]{2,1,0:T(2,128)(2,1)} reshape(bf16[256,16,64]{2,1,0:T(8,128)(2,1)S(1)} %bitcast.64) | data formatting | bytes 1048576
  79.6 3.7 %all-to-all-start.2 = ((bf16[8,2,16384]{2,1,0:T(2,128)(2,1)}), bf16[8,2,16384]{2,1,0:T(2,128)(2,1)S(1)}, u32[]{:S(2)}, u32[]{:S(2)}) async-start(bf16[8,2,16384]{2,1,0:T(2,128)(2,1)} %reshape.32), calls=%async_computation.2 | async-start | bytes 1048576 | tf_op jit(solution)/shard_map/all_to_all | solution.py:55
  83.3 0.0 copy-done.5
  83.3 0.4 fusion.13
  83.8 9.3 %all-to-all-done.2 = bf16[8,2,16384]{2,1,0:T(2,128)(2,1)S(1)} async-done(((bf16[8,2,16384]{2,1,0:T(2,128)(2,1)}), bf16[8,2,16384]{2,1,0:T(2,128)(2,1)S(1)}, u32[]{:S(2)}, u32[]{:S(2)}) %all-to-all-start.2) | async-done | bytes 524320 | tf_op jit(solution)/shard_map/all_to_all | solution.py:55
  93.0 0.7 reshape.33
  93.7 0.2 convert_bitcast_fusion
  93.9 0.2 fusion.19
  94.1 0.4 multiply_reduce_fusion
  94.5 0.0 copy-start.3
  94.5 0.3 copy.31
  94.8 0.4 copy-done.3
  95.2 0.0 copy-start.2
  95.2 0.5 fusion.2
  95.6 0.3 copy-done.2
  95.9 1.3 %fusion.17 = bf16[32,64,128]{2,1,0:T(8,128)(2,1)} fusion(f32[32,64,128]{2,1,0:T(8,128)S(1)} %fusion.13, bf16[32,64,128]{1,2,0:T(8,128)(2,1)S(1)} %fusion.2, bf16[128,128]{1,0:T(8,128)(2,1)S(1)} %copy-done.2), kind=kOutput, calls=%fused_computation.25 | convolution fusion | flops 67633152 | bytes 2129920 | tf_op jit(solution)/shard_map/ijd,dc->ijc/dot_general | solution.py:35
  (2 shorter events, 0.0 us)
Async XLA Ops:
  6.5 1.0 %copy-start = (bf16[32,64,128]{2,1,0:T(8,128)(2,1)S(1)}, bf16[32,64,128]{2,1,0:T(8,128)(2,1)}, u32[]{:S(2)}) copy-start(bf16[32,64,128]{2,1,0:T(8,128)(2,1)} %param.8) | copy-start | bytes 1572868
  6.5 68.3 %all-gather.2.cloned.1.call-start = ((), (), s32[]{:S(2)}) async-start(), calls=%async_computation.3 | async-start | bytes 2621440 | tf_op jit(solution)/shard_map/all_gather | solution.py:50
  27.5 2.1 %copy-start.1 = (bf16[128,128]{1,0:T(8,128)(2,1)S(1)}, bf16[128,128]{1,0:T(8,128)(2,1)}, u32[]{:S(2)}) copy-start(bf16[128,128]{1,0:T(8,128)(2,1)} %param.10) | copy-start | bytes 98308
  27.9 2.0 %copy-start.4 = (bf16[128,128]{1,0:T(8,128)(2,1)S(1)}, bf16[128,128]{1,0:T(8,128)(2,1)}, u32[]{:S(2)}) copy-start(bf16[128,128]{1,0:T(8,128)(2,1)} %param.12) | copy-start | bytes 98308
  77.2 6.2 %copy-start.5 = (bf16[128,128]{1,0:T(8,128)(2,1)S(1)}, bf16[128,128]{1,0:T(8,128)(2,1)}, u32[]{:S(2)}) copy-start(bf16[128,128]{1,0:T(8,128)(2,1)} %param.15) | copy-start | bytes 98308
  79.6 13.4 %all-to-all-start.2 = ((bf16[8,2,16384]{2,1,0:T(2,128)(2,1)}), bf16[8,2,16384]{2,1,0:T(2,128)(2,1)S(1)}, u32[]{:S(2)}, u32[]{:S(2)}) async-start(bf16[8,2,16384]{2,1,0:T(2,128)(2,1)} %reshape.32), calls=%async_computation.2 | async-start | bytes 1048576 | tf_op jit(solution)/shard_map/all_to_all | solution.py:55
  94.5 0.7 copy-start.3
  95.2 0.8 copy-start.2
Sparse Core Ops, SparseCore 0:
  29.7 45.0 all-gather.1
where the time goes:
time: 105 us; the launch traced here: 104 us
  waiting for transfers between devices  38.2 us (36%)
  blocking collectives  26.8 us (26%)
  between operations  13.6 us (13%)
  local copies, waits for them, and re-layouts  13.5 us (13%)
  matrix products  6.96 us (7%)
  starting transfers between devices  3.68 us (4%)
  other arithmetic  1.27 us (1%)
    all_gather x1, waiting for transfers between devices, on_device(): lax.all_gather(left_lines, 'pc', axis=1, tiled=True)  28.9 us
    all_to_all x1, blocking collectives, on_device(): lax.all_to_all(left, 'pr', split_axis=2, concat_axis=0, tiled=True)  14.7 us
    all_to_all x1, blocking collectives, on_device(): lax.all_to_all(right, 'pr', split_axis=2, concat_axis=0, tiled=True)  12.1 us
    all_to_all x1, waiting for transfers between devices, on_device(): mixed = lax.all_to_all(strip, 'pr', split_axis=0, concat_axis=2, tiled=True)  9.25 us
    unnamed x18, local copies, waits for them, and re-layouts  6.59 us
    all_to_all x1, starting transfers between devices, on_device(): mixed = lax.all_to_all(strip, 'pr', split_axis=0, concat_axis=2, tiled=True)  3.67 us
    convert_element_type x2, local copies, waits for them, and re-layouts, make_factors(): return (pair_in, left.astype(jnp.bfloat16), right.astype(jnp.bfloat16))  3.24 us
    dot_general x1, matrix products, on_device(): jnp.einsum('kid,kjd->ijd', lax.all_gather(left_lines, 'pc', axis=1, tiled...  2.35 us
  transfers between devices with their start and end apart: 2, of which 2 were waited for; matrix products, arithmetic and copies ran while one was open for 4% of the time, Pallas kernels for 0%

commit v1 on v0

--- a/solution.py
+++ b/solution.py
@@ -2,6 +2,24 @@
 import jax.numpy as jnp
 from jax import lax
 from jax.sharding import PartitionSpec as P
+
+
+def work_around(value, axis, dim, apply, out_dim):
+    size, index, rows = (lax.axis_size(axis), lax.axis_index(axis), value.shape[dim])
+    right = [(i, (i + 1) % size) for i in range(size)]
+    held, out = (value, None)
+    for step in range(size):
+        owner = (index - step) % size
+        coming = lax.ppermute(held, axis, right) if step < size - 1 else None
+        made = apply(held, owner * rows)
+        length = made.shape[out_dim]
+        if out is None:
+            out = jnp.zeros(
+                (*made.shape[:out_dim], size * length, *made.shape[out_dim + 1 :]), made.dtype
+            )
+        out = lax.dynamic_update_slice_in_dim(out, made, owner * length, axis=out_dim)
+        held = coming
+    return out
 
 
 def unit_channels(values, channel_gain):
@@ -45,11 +63,14 @@
         lax.all_to_all(left, "pr", split_axis=2, concat_axis=0, tiled=True),
         lax.all_to_all(right, "pr", split_axis=2, concat_axis=0, tiled=True),
     )
-    strip = jnp.einsum(
-        "kid,kjd->ijd",
-        lax.all_gather(left_lines, "pc", axis=1, tiled=True),
-        right_lines,
-        preferred_element_type=jnp.float32,
+    strip = work_around(
+        left_lines,
+        "pc",
+        1,
+        lambda own_block, start: jnp.einsum(
+            "kid,kjd->ijd", own_block, right_lines, preferred_element_type=jnp.float32
+        ),
+        0,
     )
     strip = (strip * count ** (-0.5)).astype(jnp.bfloat16)
     mixed = lax.all_to_all(strip, "pr", split_axis=0, concat_axis=2, tiled=True)

time: 105 us -> 93.3 us (0.89)
  blocking collectives: 26.8 us -> 0 us
  starting transfers between devices: 3.68 us -> 19.4 us
  between operations: 13.6 us -> 0.24 us
  local copies, waits for them, and re-layouts: 13.5 us -> 25.5 us
  waiting for transfers between devices: 38.2 us -> 30.1 us
  matrix products: 6.96 us -> 14.5 us
  other arithmetic: 1.27 us -> 2.42 us
    all_gather x1 -> x0, waiting for transfers between devices: 28.9 us -> none  [on_device(): lax.all_gather(left_lines, 'pc', axis=1, tiled=True)]
    all_to_all x2 -> x0, blocking collectives: 26.8 us -> none  [the longest x1 14.7 us: on_device(): lax.all_to_all(left, 'pr', split_axis=2, concat_axis=0, tiled=True)]
    all_to_all x0 -> x2, waiting for transfers between devices: none -> 14.6 us  [the longest x1 8.46 us: on_device(): lax.all_to_all(left, 'pr', split_axis=2, concat_axis=0, tiled=True)]
    all_to_all x0 -> x2, starting transfers between devices: none -> 8.68 us  [the longest x1 5.18 us: on_device(): lax.all_to_all(left, 'pr', split_axis=2, concat_axis=0, tiled=True)]
    transpose x0 -> x4, local copies, waits for them, and re-layouts: none -> 6.54 us  [on_device(): jnp.einsum('kid,kjd->ijd', own_block, right_lines, preferred_element_type...]
    ppermute x0 -> x3, waiting for transfers between devices: none -> 6.2 us  [work_around(): coming = lax.ppermute(held, axis, right) if step < size - 1 else None]
    dot_general x1 -> x4, matrix products: 2.35 us -> 7.66 us  [on_device(): jnp.einsum('kid,kjd->ijd', own_block, right_lines, preferred_element_type...]
    all_to_all x1, starting transfers between devices: 3.67 us -> 8.61 us  [on_device(): mixed = lax.all_to_all(strip, 'pr', split_axis=0, concat_axis=2, tiled=True)]
  transfers between devices with their start and end apart: 2 -> 6, of which waited for: 2 -> 6; matrix products, arithmetic and copies ran while one was open for 4% -> 23% of each run, Pallas kernels for 0% -> 0%
where the time goes in v1:
time: 93.3 us; the launch traced here: 92.1 us
  waiting for transfers between devices  30.1 us (32%)
  local copies, waits for them, and re-layouts  25.5 us (27%)
  starting transfers between devices  19.4 us (21%)
  matrix products  14.5 us (16%)
  other arithmetic  2.42 us (3%)
    unnamed x22, local copies, waits for them, and re-layouts  10.6 us
    all_to_all x1, waiting for transfers between devices, on_device(): mixed = lax.all_to_all(strip, 'pr', split_axis=0, concat_axis=2, tiled=True)  9.27 us
    all_to_all x1, starting transfers between devices, on_device(): mixed = lax.all_to_all(strip, 'pr', split_axis=0, concat_axis=2, tiled=True)  8.61 us
    all_to_all x1, waiting for transfers between devices, on_device(): lax.all_to_all(left, 'pr', split_axis=2, concat_axis=0, tiled=True)  8.46 us
    dot_general x4, matrix products, on_device(): jnp.einsum('kid,kjd->ijd', own_block, right_lines, preferred_element_type...  7.66 us
    transpose x4, local copies, waits for them, and re-layouts, on_device(): jnp.einsum('kid,kjd->ijd', own_block, right_lines, preferred_element_type...  6.54 us
    ppermute x3, waiting for transfers between devices, work_around(): coming = lax.ppermute(held, axis, right) if step < size - 1 else None  6.2 us
    all_to_all x1, waiting for transfers between devices, on_device(): lax.all_to_all(right, 'pr', split_axis=2, concat_axis=0, tiled=True)  6.15 us
  transfers between devices with their start and end apart: 6, of which 6 were waited for; matrix products, arithmetic and copies ran while one was open for 23% of the time, Pallas kernels for 0%

profile of v1, /device:TPU:0, one launch (start us, length us, event | category | flops | bytes accessed | tf_op | source)
XLA Modules:
  0.0 92.1 jit_solution(16892351249505732541)
XLA Ops:
  0.0 0.0 copy-start
  0.0 1.0 %copy-done = bf16[32,64,128]{2,1,0:T(8,128)(2,1)S(1)} copy-done((bf16[32,64,128]{2,1,0:T(8,128)(2,1)S(1)}, bf16[32,64,128]{2,1,0:T(8,128)(2,1)}, u32[]{:S(2)}) %copy-start) | copy-done | bytes 524312
  1.0 1.0 %fusion.21 = f32[32,64,128]{2,1,0:T(8,128)S(1)} fusion(bf16[32,64,128]{2,1,0:T(8,128)(2,1)S(1)} %copy-done, bf16[128,128]{1,0:T(8,128)(2,1)} %param.9), kind=kOutput, calls=%fused_computation.33 | convolution fusion | flops 67108864 | bytes 1605632 | tf_op jit(solution)/shard_map/ijc,cd->ijd/dot_general | solution.py:35
  2.1 1.2 %fusion.14 = bf16[32,64,128]{2,1,0:T(8,128)(2,1)S(1)} fusion(f32[32,64,128]{2,1,0:T(8,128)S(1)} %fusion.21, bf16[32,64,128]{2,1,0:T(8,128)(2,1)S(1)} %copy-done, bf16[128,128]{1,0:T(8,128)(2,1)} %param.11), kind=kOutput, calls=%fused_computation.22 | convolution fusion | flops 68419584 | bytes 2129920 | tf_op jit(solution)/shard_map/ijc,cd->ijd/dot_general | solution.py:37
  3.3 0.0 copy-start.3
  3.3 1.6 %copy.30 = bf16[32,64,128]{1,0,2:T(8,128)(2,1)S(1)} copy(bf16[32,64,128]{2,1,0:T(8,128)(2,1)S(1)} %fusion.14) | data formatting | bytes 1048576 | tf_op jit(solution)/shard_map/convert_element_type | solution.py:43
  4.9 1.5 %reshape.30 = bf16[8,2,16384]{2,1,0:T(2,128)(2,1)} reshape(bf16[128,32,64]{2,1,0:T(8,128)(2,1)S(1)} %bitcast.75) | data formatting | bytes 1048576
  6.4 5.2 %all-to-all-start.1 = ((bf16[8,2,16384]{2,1,0:T(2,128)(2,1)}), bf16[8,2,16384]{2,1,0:T(2,128)(2,1)S(1)}, u32[]{:S(2)}, u32[]{:S(2)}) async-start(bf16[8,2,16384]{2,1,0:T(2,128)(2,1)} %reshape.30), calls=%async_computation.1 | async-start | bytes 1048576 | tf_op jit(solution)/shard_map/all_to_all | solution.py:63
  11.6 0.0 copy-done.3
  11.6 1.2 %fusion.24 = f32[32,64,128]{2,1,0:T(8,128)} fusion(bf16[32,64,128]{2,1,0:T(8,128)(2,1)S(1)} %copy-done, bf16[128,128]{1,0:T(8,128)(2,1)S(1)} %copy-done.3), kind=kOutput, calls=%fused_computation.36 | convolution fusion | flops 67108864 | bytes 1605632 | tf_op jit(solution)/shard_map/ijc,cd->ijd/dot_general | solution.py:39
  12.9 8.5 %all-to-all-done.1 = bf16[8,2,16384]{2,1,0:T(2,128)(2,1)S(1)} async-done(((bf16[8,2,16384]{2,1,0:T(2,128)(2,1)}), bf16[8,2,16384]{2,1,0:T(2,128)(2,1)S(1)}, u32[]{:S(2)}, u32[]{:S(2)}) %all-to-all-start.1) | async-done | bytes 524320 | tf_op jit(solution)/shard_map/all_to_all | solution.py:63
  21.3 0.7 reshape.31
  22.0 0.0 copy-start.6
  22.0 0.4 copy.32
  22.4 0.8 copy.34
  23.3 0.0 copy-start.1
  23.3 1.6 %collective-permute-start = (bf16[256,64,16]{0,1,2:T(8,128)(2,1)S(1)}, bf16[256,64,16]{0,1,2:T(8,128)(2,1)}, u32[]{:S(2)}, u32[]{:S(2)}) collective-permute-start(bf16[256,64,16]{0,1,2:T(8,128)(2,1)S(1)} %copy.34), channel_id=1, source_target_pairs={{0,1},{1,2},{2,3},{3,0},{4,5},{5,6},{6,7},{7,4},{8,9},{9,10},{10,1... | collective-permute-start | bytes 1572872 | tf_op jit(solution)/shard_map/ppermute | solution.py:13
  24.9 0.0 copy-done.6
  24.9 1.6 %fusion.15 = bf16[32,64,128]{2,1,0:T(8,128)(2,1)S(1)} fusion(f32[32,64,128]{2,1,0:T(8,128)} %fusion.24, bf16[32,64,128]{2,1,0:T(8,128)(2,1)S(1)} %copy-done, bf16[128,128]{1,0:T(8,128)(2,1)S(1)} %copy-done.6), kind=kOutput, calls=%fused_computation.23 | convolution fusion | flops 68419584 | bytes 2129920 | tf_op jit(solution)/shard_map/ijc,cd->ijd/dot_general | solution.py:41
  26.6 0.0 copy-done.1
  26.6 1.6 %copy.27 = bf16[32,64,128]{1,0,2:T(8,128)(2,1)S(1)} copy(bf16[32,64,128]{2,1,0:T(8,128)(2,1)S(1)} %fusion.15) | data formatting | bytes 1048576 | tf_op jit(solution)/shard_map/convert_element_type | solution.py:43
  28.2 1.5 %reshape.28 = bf16[8,2,16384]{2,1,0:T(2,128)(2,1)} reshape(bf16[128,32,64]{2,1,0:T(8,128)(2,1)S(1)} %bitcast.76) | data formatting | bytes 1048576
  29.7 3.5 %all-to-all-start = ((bf16[8,2,16384]{2,1,0:T(2,128)(2,1)}), bf16[8,2,16384]{2,1,0:T(2,128)(2,1)S(1)}, u32[]{:S(2)}, u32[]{:S(2)}) async-start(bf16[8,2,16384]{2,1,0:T(2,128)(2,1)} %reshape.28), calls=%async_computation | async-start | bytes 1048576 | tf_op jit(solution)/shard_map/all_to_all | solution.py:64
  33.2 3.5 %collective-permute-done = bf16[256,64,16]{0,1,2:T(8,128)(2,1)} collective-permute-done((bf16[256,64,16]{0,1,2:T(8,128)(2,1)S(1)}, bf16[256,64,16]{0,1,2:T(8,128)(2,1)}, u32[]{:S(2)}, u32[]{:S(2)}) %collective-permute-start) | collective-permute-done | bytes 524320 | tf_op jit(solution)/shard_map/ppermute | solution.py:13
  36.7 0.0 collective-permute-start.1
  36.7 6.1 %all-to-all-done = bf16[8,2,16384]{2,1,0:T(2,128)(2,1)S(1)} async-done(((bf16[8,2,16384]{2,1,0:T(2,128)(2,1)}), bf16[8,2,16384]{2,1,0:T(2,128)(2,1)S(1)}, u32[]{:S(2)}, u32[]{:S(2)}) %all-to-all-start) | async-done | bytes 524320 | tf_op jit(solution)/shard_map/all_to_all | solution.py:64
  42.9 0.7 reshape.29
  43.5 0.4 copy.29
  43.9 0.8 copy.33
  44.8 1.3 %convolution_bitcast_fusion.3 = f32[64,64,16]{0,1,2:T(8,128)S(1)} fusion(bf16[256,64,16]{0,1,2:T(8,128)(2,1)S(1)} %copy.33, bf16[256,64,16]{0,1,2:T(8,128)(2,1)} %copy-done.1), kind=kOutput, calls=%fused_computation.28 | convolution fusion | flops 33554432 | bytes 1310720 | tf_op jit(solution)/shard_map/kid,kjd->ijd/dot_general | solution.py:70
  46.1 1.0 %copy.35 = f32[64,64,16]{1,2,0:T(8,128)} copy(f32[64,64,16]{0,1,2:T(8,128)S(1)} %convolution_bitcast_fusion.3) | data formatting | bytes 524288 | tf_op jit(solution)/shard_map/kid,kjd->ijd/transpose | solution.py:70
  47.1 0.0 copy-start.2
  47.1 0.1 broadcast_in_dim.2
  47.3 0.9 copy-done.2
  48.2 1.3 %collective-permute-done.1 = bf16[256,64,16]{0,1,2:T(8,128)(2,1)} collective-permute-done((bf16[256,64,16]{0,1,2:T(8,128)(2,1)}, bf16[256,64,16]{0,1,2:T(8,128)(2,1)}, u32[]{:S(2)}, u32[]{:S(2)}) %collective-permute-start.1) | collective-permute-done | bytes 524320 | tf_op jit(solution)/shard_map/ppermute | solution.py:13
  49.6 0.5 collective-permute-start.2
  50.0 2.1 %convolution_bitcast_fusion.2 = f32[64,64,16]{0,1,2:T(8,128)} fusion(bf16[256,64,16]{0,1,2:T(8,128)(2,1)S(1)} %copy.33, bf16[256,64,16]{0,1,2:T(8,128)(2,1)} %collective-permute-done), kind=kOutput, calls=%fused_computation.27 | convolution fusion | flops 33554432 | bytes 1310720 | tf_op jit(solution)/shard_map/kid,kjd->ijd/dot_general | solution.py:70
  52.2 2.1 %copy.38 = f32[64,64,16]{1,2,0:T(8,128)} copy(f32[64,64,16]{0,1,2:T(8,128)} %convolution_bitcast_fusion.2) | data formatting | bytes 524288 | tf_op jit(solution)/shard_map/kid,kjd->ijd/transpose | solution.py:70
  54.3 1.1 %constant_dynamic-update-slice_fusion.2 = f32[256,64,16]{1,2,0:T(8,128)S(1)} fusion(f32[256,64,16]{1,2,0:T(8,128)S(1)} %constant_dynamic-update-slice_fusion.3, f32[64,64,16]{1,2,0:T(8,128)} %copy.38, s32[]{:T(128)S(6)} %select_n.34), kind=kLoop, calls=%fused_computation.42 | loop fusion | bytes 786436 | tf_op jit(solution)/shard_map/dynamic_update_slice | solution.py:20
  55.3 2.1 %convolution_bitcast_fusion.1 = f32[64,64,16]{0,1,2:T(8,128)} fusion(bf16[256,64,16]{0,1,2:T(8,128)(2,1)S(1)} %copy.33, bf16[256,64,16]{0,1,2:T(8,128)(2,1)} %collective-permute-done.1), kind=kOutput, calls=%fused_computation.26 | convolution fusion | flops 33554432 | bytes 1310720 | tf_op jit(solution)/shard_map/kid,kjd->ijd/dot_general | solution.py:70
  57.4 2.1 %copy.40 = f32[64,64,16]{1,2,0:T(8,128)} copy(f32[64,64,16]{0,1,2:T(8,128)} %convolution_bitcast_fusion.1) | data formatting | bytes 524288 | tf_op jit(solution)/shard_map/kid,kjd->ijd/transpose | solution.py:70
  59.5 1.1 %constant_dynamic-update-slice_fusion.1 = f32[256,64,16]{1,2,0:T(8,128)S(1)} fusion(f32[256,64,16]{1,2,0:T(8,128)S(1)} %constant_dynamic-update-slice_fusion.2, f32[64,64,16]{1,2,0:T(8,128)} %copy.40, s32[]{:T(128)S(6)} %select_n.36), kind=kLoop, calls=%fused_computation.41 | loop fusion | bytes 786436 | tf_op jit(solution)/shard_map/dynamic_update_slice | solution.py:20
  60.6 1.4 %collective-permute-done.2 = bf16[256,64,16]{0,1,2:T(8,128)(2,1)} collective-permute-done((bf16[256,64,16]{0,1,2:T(8,128)(2,1)}, bf16[256,64,16]{0,1,2:T(8,128)(2,1)}, u32[]{:S(2)}, u32[]{:S(2)}) %collective-permute-start.2) | collective-permute-done | bytes 524320 | tf_op jit(solution)/shard_map/ppermute | solution.py:13
  62.0 2.1 %convolution_bitcast_fusion = f32[64,64,16]{0,1,2:T(8,128)} fusion(bf16[256,64,16]{0,1,2:T(8,128)(2,1)S(1)} %copy.33, bf16[256,64,16]{0,1,2:T(8,128)(2,1)} %collective-permute-done.2), kind=kOutput, calls=%fused_computation.25 | convolution fusion | flops 33554432 | bytes 1310720 | tf_op jit(solution)/shard_map/kid,kjd->ijd/dot_general | solution.py:70
  64.1 1.3 %copy.42 = f32[64,64,16]{1,2,0:T(8,128)S(1)} copy(f32[64,64,16]{0,1,2:T(8,128)} %convolution_bitcast_fusion) | data formatting | bytes 524288 | tf_op jit(solution)/shard_map/kid,kjd->ijd/transpose | solution.py:70
  65.5 1.2 %fusion.26 = bf16[256,16,64]{2,1,0:T(8,128)(2,1)} fusion(f32[256,64,16]{1,2,0:T(8,128)S(1)} %constant_dynamic-update-slice_fusion), kind=kLoop, calls=%fused_computation.44 | loop fusion | flops 524288 | bytes 1572864
  66.6 0.0 copy-start.7
  66.6 3.0 %reshape.32 = bf16[8,2,16384]{2,1,0:T(2,128)(2,1)} reshape(bf16[256,16,64]{2,1,0:T(8,128)(2,1)} %fusion.26) | data formatting | bytes 1048576
  69.6 8.6 %all-to-all-start.2 = ((bf16[8,2,16384]{2,1,0:T(2,128)(2,1)}), bf16[8,2,16384]{2,1,0:T(2,128)(2,1)S(1)}, u32[]{:S(2)}, u32[]{:S(2)}) async-start(bf16[8,2,16384]{2,1,0:T(2,128)(2,1)} %reshape.32), calls=%async_computation.2 | async-start | bytes 1048576 | tf_op jit(solution)/shard_map/all_to_all | solution.py:76
  78.3 0.0 copy-done.7
  78.3 0.4 fusion.13
  78.7 9.3 %all-to-all-done.2 = bf16[8,2,16384]{2,1,0:T(2,128)(2,1)S(1)} async-done(((bf16[8,2,16384]{2,1,0:T(2,128)(2,1)}), bf16[8,2,16384]{2,1,0:T(2,128)(2,1)S(1)}, u32[]{:S(2)}, u32[]{:S(2)}) %all-to-all-start.2) | async-done | bytes 524320 | tf_op jit(solution)/shard_map/all_to_all | solution.py:76
  88.0 0.7 reshape.33
  88.6 0.2 convert_bitcast_fusion
  88.8 0.2 fusion.17
  89.1 0.4 multiply_reduce_fusion
  89.5 0.0 copy-start.5
  89.5 0.3 copy.43
  89.8 0.4 copy-done.5
  90.1 0.0 copy-start.4
  90.1 0.5 fusion.2
  90.6 0.3 copy-done.4
  90.9 1.3 %fusion.16 = bf16[32,64,128]{2,1,0:T(8,128)(2,1)} fusion(f32[32,64,128]{2,1,0:T(8,128)S(1)} %fusion.13, bf16[32,64,128]{1,2,0:T(8,128)(2,1)S(1)} %fusion.2, bf16[128,128]{1,0:T(8,128)(2,1)S(1)} %copy-done.4), kind=kOutput, calls=%fused_computation.24 | convolution fusion | flops 67633152 | bytes 2129920 | tf_op jit(solution)/shard_map/ijd,dc->ijc/dot_general | solution.py:53
  (4 shorter events, 0.1 us)
Async XLA Ops:
  0.0 1.0 %copy-start = (bf16[32,64,128]{2,1,0:T(8,128)(2,1)S(1)}, bf16[32,64,128]{2,1,0:T(8,128)(2,1)}, u32[]{:S(2)}) copy-start(bf16[32,64,128]{2,1,0:T(8,128)(2,1)} %param.8) | copy-start | bytes 1572868
  3.3 8.3 %copy-start.3 = (bf16[128,128]{1,0:T(8,128)(2,1)S(1)}, bf16[128,128]{1,0:T(8,128)(2,1)}, u32[]{:S(2)}) copy-start(bf16[128,128]{1,0:T(8,128)(2,1)} %param.10) | copy-start | bytes 98308
  6.4 14.9 %all-to-all-start.1 = ((bf16[8,2,16384]{2,1,0:T(2,128)(2,1)}), bf16[8,2,16384]{2,1,0:T(2,128)(2,1)S(1)}, u32[]{:S(2)}, u32[]{:S(2)}) async-start(bf16[8,2,16384]{2,1,0:T(2,128)(2,1)} %reshape.30), calls=%async_computation.1 | async-start | bytes 1048576 | tf_op jit(solution)/shard_map/all_to_all | solution.py:63
  22.0 2.9 %copy-start.6 = (bf16[128,128]{1,0:T(8,128)(2,1)S(1)}, bf16[128,128]{1,0:T(8,128)(2,1)}, u32[]{:S(2)}) copy-start(bf16[128,128]{1,0:T(8,128)(2,1)} %param.12) | copy-start | bytes 98308
  23.3 3.3 %copy-start.1 = (bf16[256,64,16]{0,1,2:T(8,128)(2,1)}, bf16[256,64,16]{0,1,2:T(8,128)(2,1)S(1)}, u32[]{:S(2)}) copy-start(bf16[256,64,16]{0,1,2:T(8,128)(2,1)S(1)} %copy.34) | copy-start | bytes 1572868
  23.3 13.4 %collective-permute-start = (bf16[256,64,16]{0,1,2:T(8,128)(2,1)S(1)}, bf16[256,64,16]{0,1,2:T(8,128)(2,1)}, u32[]{:S(2)}, u32[]{:S(2)}) collective-permute-start(bf16[256,64,16]{0,1,2:T(8,128)(2,1)S(1)} %copy.34), channel_id=1, source_target_pairs={{0,1},{1,2},{2,3},{3,0},{4,5},{5,6},{6,7},{7,4},{8,9},{9,10},{10,1... | collective-permute-start | bytes 1572872 | tf_op jit(solution)/shard_map/ppermute | solution.py:13
  29.7 13.2 %all-to-all-start = ((bf16[8,2,16384]{2,1,0:T(2,128)(2,1)}), bf16[8,2,16384]{2,1,0:T(2,128)(2,1)S(1)}, u32[]{:S(2)}, u32[]{:S(2)}) async-start(bf16[8,2,16384]{2,1,0:T(2,128)(2,1)} %reshape.28), calls=%async_computation | async-start | bytes 1048576 | tf_op jit(solution)/shard_map/all_to_all | solution.py:64
  36.7 12.9 %collective-permute-start.1 = (bf16[256,64,16]{0,1,2:T(8,128)(2,1)}, bf16[256,64,16]{0,1,2:T(8,128)(2,1)}, u32[]{:S(2)}, u32[]{:S(2)}) collective-permute-start(bf16[256,64,16]{0,1,2:T(8,128)(2,1)} %collective-permute-done), channel_id=1, source_target_pairs={{0,1},{1,2},{2,3},{3,0},{4,5},{5,6},{6,7},{7,4},{8,9},{9,10},{10,1... | collective-permute-start | bytes 1572872 | tf_op jit(solution)/shard_map/ppermute | solution.py:13
  47.1 1.0 %copy-start.2 = (f32[64,64,16]{1,2,0:T(8,128)S(1)}, f32[64,64,16]{1,2,0:T(8,128)}, u32[]{:S(2)}) copy-start(f32[64,64,16]{1,2,0:T(8,128)} %copy.35) | copy-start | bytes 786436
  49.6 12.4 %collective-permute-start.2 = (bf16[256,64,16]{0,1,2:T(8,128)(2,1)}, bf16[256,64,16]{0,1,2:T(8,128)(2,1)}, u32[]{:S(2)}, u32[]{:S(2)}) collective-permute-start(bf16[256,64,16]{0,1,2:T(8,128)(2,1)} %collective-permute-done.1), channel_id=1, source_target_pairs={{0,1},{1,2},{2,3},{3,0},{4,5},{5,6},{6,7},{7,4},{8,9},{9,10},{10,1... | collective-permute-start | bytes 1572872 | tf_op jit(solution)/shard_map/ppermute | solution.py:13
  66.6 11.6 %copy-start.7 = (bf16[128,128]{1,0:T(8,128)(2,1)S(1)}, bf16[128,128]{1,0:T(8,128)(2,1)}, u32[]{:S(2)}) copy-start(bf16[128,128]{1,0:T(8,128)(2,1)} %param.15) | copy-start | bytes 98308
  69.6 18.3 %all-to-all-start.2 = ((bf16[8,2,16384]{2,1,0:T(2,128)(2,1)}), bf16[8,2,16384]{2,1,0:T(2,128)(2,1)S(1)}, u32[]{:S(2)}, u32[]{:S(2)}) async-start(bf16[8,2,16384]{2,1,0:T(2,128)(2,1)} %reshape.32), calls=%async_computation.2 | async-start | bytes 1048576 | tf_op jit(solution)/shard_map/all_to_all | solution.py:76
  89.5 0.7 copy-start.5
  90.1 0.8 copy-start.4
